TPU v7x, 32 devices: a whole 2x2x4 slice. The times are simulated.
32 devices in a mesh: freq: 8 (over z, y), rows: 4 (over x, core).
Axes of the slice: x: 2, y: 2, z: 4, core: 2. Of those that a mesh axis runs over, the one named last changes fastest.
Arguments:
- wavefield: bfloat16 [10240, 32, 1024], P('freq', 'rows'), may hold values from -6 to 6
- u_factors: bfloat16 [2, 16, 4, 256, 512], P(None, 'freq', 'rows'), may hold values from -0.25 to 0.25
- v_factors: bfloat16 [2, 16, 4, 512, 256], P(None, 'freq', 'rows'), may hold values from -0.375 to 0.375
- tile_ranks: int32 [16, 4, 40], P('freq', 'rows'), may hold values from 1 to 64, as said below
- tile_offsets: int32 [16, 4, 40], P('freq', 'rows'), may hold values from 0 to 511, as said below
Outputs:
- convolved: bfloat16 [1024, 32, 1024], P(('rows', 'freq'))
Inputs may be any that keep to these rules, and one draw needn't show every extreme that they name: tile_ranks[k, i, j] is the rank of tile (i, j) of frequency k; the ranks of one tile row sum to at most 512, exactly 512 on some row of every draw, and every tile row has a tile of rank 64. tile_offsets[k, i, j] is the sum of tile_ranks[k, i, j2] over j2 < j.
All inputs are finite; a program needn't handle non-finite values.
Results may differ from a plain program's by a relative error of at most 0.0072.
Values may be sent and summed in bfloat16 or wider, within the bound.
A program may use at most 128 MiB of HBM per device.

v0:
```python
import functools
import math

import jax
import jax.numpy as jnp
from jax import lax
from jax.sharding import PartitionSpec as P

RANK_MAX = 64


def spectral_tables(freq_count, sample_count):
    freq_bins = jnp.arange(freq_count, dtype=jnp.int32) + 1
    sample_index = jnp.arange(sample_count, dtype=jnp.int32)
    phase_int = freq_bins[:, None] * sample_index[None, :] % sample_count
    angles = phase_int.astype(jnp.float32) * (2.0 * math.pi / sample_count)
    cosine = jnp.cos(angles)
    minus_sine = -jnp.sin(angles)
    stacked = jnp.stack([cosine, minus_sine], axis=1)
    forward = (stacked / math.sqrt(sample_count)).astype(jnp.bfloat16)
    inverse = (stacked / math.sqrt(freq_count)).astype(jnp.bfloat16)
    return (forward, inverse)


def tile_windows(v_row, u_row, starts, rank_max):
    columns = starts.shape[0]
    slot_index = (starts[:, None] + jnp.arange(rank_max, dtype=jnp.int32)[None, :]).reshape(-1)
    v_padded = jnp.pad(v_row, ((0, 0), (0, rank_max), (0, 0)))
    u_padded = jnp.pad(u_row, ((0, 0), (0, 0), (0, rank_max)))
    v_win = jnp.take(v_padded, slot_index, axis=1).reshape(2, columns, rank_max, v_row.shape[2])
    u_win = jnp.take(u_padded, slot_index, axis=2).reshape(2, u_row.shape[1], columns, rank_max)
    return (v_win, u_win)


def slot_lookup(starts, counts, rank_max, slot_count):
    position = jnp.arange(slot_count, dtype=jnp.int32)
    started = starts[:, None, :] <= position[None, :, None]
    owner_tile = jnp.sum(started.astype(jnp.int32), axis=2) - 1
    first_slot = jnp.max(jnp.where(started, starts[:, None, :], 0), axis=2)
    within = position[None, :] - first_slot
    live_slot = position[None, :] < (starts[:, -1] + counts[:, -1])[:, None]
    flat_index = jnp.where(live_slot, owner_tile * rank_max + within, 0)
    return (flat_index, live_slot)


def take_slots(values, chosen):
    return jnp.take(values, chosen, axis=1)


def per_device(wavefield, u_factors, v_factors, tile_ranks, tile_offsets):
    rec_dev, src_dev, samples = wavefield.shape
    freq_dev = u_factors.shape[1]
    rows_dev = u_factors.shape[2]
    tile_size = u_factors.shape[3]
    slot_count = u_factors.shape[4]
    freq_group = lax.axis_size("freq")
    row_group = lax.axis_size("rows")
    freqs = freq_dev * freq_group
    receivers = rec_dev * freq_group
    columns = receivers // tile_size
    sources = src_dev * row_group
    forward, inverse = spectral_tables(freqs, samples)
    spectrum = jnp.einsum("kct,rst->kcrs", forward, wavefield, preferred_element_type=jnp.float32)
    spectrum = spectrum.astype(jnp.bfloat16).reshape(freqs, 2, rec_dev * src_dev)
    windows = jax.vmap(
        functools.partial(tile_windows, rank_max=RANK_MAX), in_axes=(1, 1, 0), out_axes=(1, 1)
    )
    rank_slots = jnp.arange(RANK_MAX, dtype=jnp.int32)
    tile_row = 0
    v_win, u_win = windows(
        v_factors[:, :, tile_row], u_factors[:, :, tile_row], tile_offsets[:, tile_row]
    )
    rank_mask = rank_slots[None, None, :] < tile_ranks[:, tile_row, :, None]
    flat_index, live_slot = slot_lookup(
        tile_offsets[:, tile_row], tile_ranks[:, tile_row], RANK_MAX, slot_count
    )
    prepared = [(v_win, u_win, rank_mask, flat_index, live_slot)]
    by_frequency = lax.all_to_all(spectrum, "freq", split_axis=0, concat_axis=2, tiled=True)
    portion = lax.all_gather(by_frequency[None], "rows", axis=0, tiled=True)
    blocks_in = portion.shape[0]
    spectra = portion.reshape(blocks_in, freq_dev, 2, columns, tile_size, src_dev)
    spectra = jnp.transpose(spectra, (1, 2, 3, 4, 0, 5)).reshape(
        freq_dev, 2, columns, tile_size, blocks_in * src_dev
    )
    tile_row = 0
    v_win, u_win, rank_mask, flat_index, live_slot = prepared[tile_row]
    quadrants = jnp.einsum(
        "afjmr,fbjrs->fabjms", v_win, spectra, preferred_element_type=jnp.float32
    )
    coeffs = jnp.stack(
        [quadrants[:, 0, 0] - quadrants[:, 1, 1], quadrants[:, 0, 1] + quadrants[:, 1, 0]], axis=1
    )
    coeffs = jnp.where(rank_mask[:, None, :, :, None], coeffs, 0.0).astype(jnp.bfloat16)
    stacked = coeffs.reshape(freq_dev, 2, columns * RANK_MAX, blocks_in * src_dev)
    packed = jax.vmap(take_slots)(stacked, flat_index)
    packed = jnp.where(live_slot[:, None, :, None], packed, jnp.zeros((), jnp.bfloat16))
    products = jnp.einsum(
        "afrk,fcks->facrs", u_factors[:, :, tile_row], packed, preferred_element_type=jnp.float32
    )
    results = [
        jnp.stack(
            [products[:, 0, 0] - products[:, 1, 1], products[:, 0, 1] + products[:, 1, 0]], axis=1
        )
    ]
    merged = jnp.stack(results, axis=2)
    bands = merged.astype(jnp.bfloat16).reshape(
        freq_dev, 2, rows_dev * tile_size, blocks_in, src_dev
    )
    bands = bands.reshape(freq_dev, 2, rows_dev * tile_size * sources)
    returned = lax.all_to_all(bands, "freq", split_axis=2, concat_axis=0, tiled=True)
    series = jnp.einsum("kcq,kct->qt", returned, inverse, preferred_element_type=jnp.float32)
    return series.astype(jnp.bfloat16).reshape(rows_dev * tile_size // freq_group, sources, samples)


def solution(mesh):
    placed = (
        P("freq", "rows", None),
        P(None, "freq", "rows", None, None),
        P(None, "freq", "rows", None, None),
        P("freq", "rows", None),
        P("freq", "rows", None),
    )
    return jax.shard_map(
        per_device,
        mesh=mesh,
        in_specs=placed,
        out_specs=P(("rows", "freq"), None, None),
        check_vma=False,
    )
```

profile of v0, /device:TPU:0, one launch (start us, length us, event | category | flops | bytes accessed | tf_op | source)
XLA Modules:
  0.0 294.8 jit_solution(15557455718139508555)
XLA Ops:
  6.5 0.0 copy-start
  6.5 0.0 all-gather.2.cloned.1.call-start
  6.5 0.3 fusion.33
  6.9 24.3 %fusion.6 = bf16[16,2,1280,8]{2,0,3,1:T(8,128)(2,1)S(1)} fusion(bf16[1280,8,1024]{2,1,0:T(8,128)(2,1)} %param.5, f32[16,1,1024]{2,0,1:T(8,128)S(1)} %get-tuple-element.14, f32[16,1,1024]{2,0,1:T(8,128)S(1)} %get-tuple-element.13), kind=kOutput, calls=%fused_computation.10 | convolution fusion | flops 671514624 | bytes 21757952 | tf_op jit(solution)/shard_map/kct,rst->kcrs/dot_general | solution.py:63
  31.2 4.5 %copy.92 = bf16[16,2,1280,8]{0,3,2,1:T(8,128)(2,1)} copy(bf16[16,2,1280,8]{2,0,3,1:T(8,128)(2,1)S(1)} %fusion.6) | data formatting | bytes 1310720 | tf_op jit(solution)/shard_map/convert_element_type | solution.py:64
  35.7 4.8 %copy.93 = bf16[16,2,10240]{2,1,0:T(2,128)(2,1)S(1)} copy(bf16[16,2,10240]{0,2,1:T(8,128)(2,1)} %bitcast.107) | data formatting | bytes 1310720 | tf_op jit(solution)/shard_map/reshape | solution.py:64
  40.5 0.0 copy-start.2
  40.5 0.0 copy-start.1
  40.5 24.9 %all_to_all.33 = bf16[16,2,10240]{2,1,0:T(2,128)(2,1)S(1)} all-to-all(bf16[16,2,10240]{2,1,0:T(2,128)(2,1)S(1)} %copy.93), channel_id=1, replica_groups=mesh['freq'=8,'rows'=4] {'freq'}, dimensions={0} | all-to-all | bytes 1310720 | tf_op jit(solution)/shard_map/all_to_all | solution.py:78
  65.5 0.4 copy.94
  65.8 1.2 broadcast_in_dim.78
  67.1 0.0 all-gather.2.cloned.1.call-update
  67.1 0.0 copy-done.2
  67.1 0.1 add.162
  67.2 0.1 add.166
  67.3 0.1 lt.123
  67.4 0.0 copy-done.1
  67.4 1.1 copy.141
  68.5 1.0 pad_bitcast_fusion
  69.5 45.7 %gather_fusion = bf16[5120,2,256]{2,1,0:T(2,128)(2,1)} fusion(bf16[2,2,576,256]{3,1,2,0:T(2,128)(2,1)S(1)} %pad_bitcast_fusion, s32[5120]{0:T(1024)S(1)} %reshape.407), kind=kCustom, calls=%fused_computation | custom fusion | bytes 10526720 | tf_op jit(solution)/shard_map/vmap(jit(_take))/gather | solution.py:30
  115.2 0.0 copy-start.3
  115.2 5.5 %copy.97 = bf16[2,2560,2,256]{3,1,2,0:T(8,128)(2,1)} copy(bf16[2,2560,2,256]{3,2,1,0:T(2,128)(2,1)} %bitcast.106) | data formatting | bytes 10485760 | tf_op jit(solution)/shard_map/vmap(jit(_take))/gather | solution.py:30
  120.7 0.0 copy-done.3
  120.7 0.1 lt.125
  120.8 0.1 lt.126
  120.9 0.2 add_reduce_fusion
  121.1 0.1 convert_reduce_fusion
  121.2 0.1 or_bitcast_fusion
  121.3 0.1 fusion.32
  121.4 0.1 iota_compare_fusion.1
  121.5 0.0 all-gather.2.cloned.1.call-done
  121.5 74.5 %reshape.404 = bf16[4,2,2,40,256,8]{5,4,3,2,1,0:T(8,128)(2,1)} reshape(bf16[4,2,2,81920]{3,2,1,0:T(2,128)(2,1)} %all-gather.2.cloned.1.call-done) | data formatting | bytes 5242880 | tf_op jit(solution)/shard_map/reshape | solution.py:81
  196.0 30.3 %copy.95 = bf16[2,2,40,256,4,8]{3,5,4,1,2,0:T(8,128)(2,1)} copy(bf16[2,2,40,256,4,8]{5,3,2,1,0,4:T(8,128)(2,1)} %bitcast.104) | data formatting | bytes 5242880 | tf_op jit(solution)/shard_map/transpose | solution.py:82
  226.3 5.3 %fusion.9 = f32[2,2,2,40,64,32]{4,5,1,2,3,0:T(8,128)S(1)} fusion(bf16[2,2,40,256,4,8]{3,5,4,1,2,0:T(8,128)(2,1)} %copy.95, bf16[2,2,40,64,256]{4,3,2,1,0:T(8,128)(2,1)} %bitcast.110, pred[2,40,64]{2,1,0:T(8,128)(4,1)S(1)} %fusion.32), kind=kOutput, calls=%fused_computation.11 | convolution fusion | flops 338165760 | bytes 10490880 | tf_op jit(solution)/shard_map/afjmr,fbjrs->fabjms/dot_general | solution.py:87
  231.6 0.6 slice_subtract_fusion
  232.2 0.3 copy.99
  232.5 0.4 sub.52
  232.9 0.3 copy.100
  233.2 0.4 add.171
  233.6 0.1 fusion.14
  233.7 4.1 %copy.103 = bf16[2,2,2560,32]{3,1,2,0:T(2,128)(2,1)} copy(bf16[2,2,2560,32]{2,3,1,0:T(8,128)(2,1)S(1)} %fusion.14) | data formatting | bytes 1310720 | tf_op jit(solution)/shard_map/convert_element_type | solution.py:93
  237.7 6.2 %gather_fusion.1 = bf16[1024,2,32]{2,1,0:T(2,128)(2,1)S(1)} fusion(bf16[2,2,2560,32]{3,1,2,0:T(2,128)(2,1)} %copy.103, s32[1024]{0:T(1024)S(1)} %bitcast.105), kind=kCustom, calls=%fused_computation.1 | custom fusion | bytes 270336 | tf_op jit(solution)/shard_map/vmap(jit(_take))/gather | solution.py:47
  244.0 0.4 copy.119
  244.4 0.1 fusion.16
  244.5 0.0 copy-done
  244.5 0.4 convolution_bitcast_fusion
  245.0 0.1 copy.108
  245.1 0.2 add.176
  245.3 0.1 copy.107
  245.4 0.2 sub.55
  245.6 0.1 pad_maximum_fusion.1
  245.7 6.9 %copy.109 = bf16[2,2,8192]{0,1,2:T(2,128)(2,1)} copy(bf16[2,2,8192]{2,0,1:T(2,128)(2,1)S(1)} %pad_maximum_fusion.1) | data formatting | bytes 131072 | tf_op jit(solution)/shard_map/stack | solution.py:101
  252.6 7.2 %reshape.427 = bf16[8,2,2048]{2,1,0:T(2,128)(2,1)S(1)} reshape(bf16[8192,2,2]{2,1,0:T(2,128)(2,1)} %bitcast.108) | data formatting | bytes 131072
  259.7 10.0 %all_to_all.34 = bf16[8,2,2048]{2,1,0:T(2,128)(2,1)S(1)} all-to-all(bf16[8,2,2048]{2,1,0:T(2,128)(2,1)S(1)} %reshape.427), channel_id=1, replica_groups=mesh['freq'=8,'rows'=4] {'freq'}, dimensions={0} | all-to-all | bytes 131072 | tf_op jit(solution)/shard_map/all_to_all | solution.py:110
  269.7 10.0 %reshape.428 = bf16[8192,2,2]{2,1,0:T(2,128)(2,1)} reshape(bf16[8,2,2048]{2,1,0:T(2,128)(2,1)S(1)} %all_to_all.34) | data formatting | bytes 131072
  279.7 6.1 %copy.124 = bf16[2,2,8,1024]{3,2,1,0:T(8,128)(2,1)S(1)} copy(bf16[2,2,8,1024]{0,1,3,2:T(2,128)(2,1)} %bitcast.109) | data formatting | bytes 131072 | tf_op jit(solution)/shard_map/all_to_all | solution.py:110
  285.8 0.1 copy.111
  285.9 2.0 bitcast_convert_fusion
  (8 shorter events, 0.1 us)
Async XLA Ops:
  6.5 238.0 %copy-start = (bf16[2,2,1,256,512]{4,3,2,1,0:T(8,128)(2,1)S(1)}, bf16[2,2,1,256,512]{4,3,2,1,0:T(8,128)(2,1)}, u32[]{:S(2)}) copy-start(bf16[2,2,1,256,512]{4,3,2,1,0:T(8,128)(2,1)} %param.6) | copy-start | bytes 3145732
  6.5 115.0 %all-gather.2.cloned.1.call-start = ((), (), s32[]{:S(2)}) async-start(), calls=%async_computation.2 | async-start | bytes 3276800 | tf_op jit(solution)/shard_map/all_gather | solution.py:79
  40.5 26.6 %copy-start.2 = (s32[2,1,40]{2,1,0:T(1,128)S(1)}, s32[2,1,40]{2,1,0:T(1,128)}, u32[]{:S(2)}) copy-start(s32[2,1,40]{2,1,0:T(1,128)} %param.9) | copy-start | bytes 964
  40.5 26.9 %copy-start.1 = (bf16[2,2,1,512,256]{4,3,2,1,0:T(8,128)(2,1)S(1)}, bf16[2,2,1,512,256]{4,3,2,1,0:T(8,128)(2,1)}, u32[]{:S(2)}) copy-start(bf16[2,2,1,512,256]{4,3,2,1,0:T(8,128)(2,1)} %param.7) | copy-start | bytes 3145732
  115.2 5.5 %copy-start.3 = (s32[2,1,40]{2,1,0:T(1,128)S(1)}, s32[2,1,40]{2,1,0:T(1,128)}, u32[]{:S(2)}) copy-start(s32[2,1,40]{2,1,0:T(1,128)} %param.8) | copy-start | bytes 964
Sparse Core Ops, SparseCore 0:
  67.2 24.1 all-gather.1
where the time goes:
time: 296 us; the launch traced here: 295 us
  local copies, waits for them, and re-layouts  212 us (72%)
  blocking collectives  34.9 us (12%)
  matrix products  32.1 us (11%)
  between operations  13.7 us (5%)
    reshape x1, local copies, waits for them, and re-layouts, per_device(): portion.reshape(blocks_in, freq_dev, 2, columns, tile_size, src_dev)  74.5 us
    gather x3, local copies, waits for them, and re-layouts, tile_windows(): jnp.take(v_padded, slot_index, axis=1)  51.3 us
    transpose x1, local copies, waits for them, and re-layouts, per_device(): jnp.transpose(spectra, (1, 2, 3, 4, 0, 5))  30.3 us
    all_to_all x1, blocking collectives, per_device(): lax.all_to_all(spectrum, 'freq', split_axis=0, concat_axis=2, tiled=True)  24.9 us
    dot_general x1, matrix products, per_device(): jnp.einsum('kct,rst->kcrs', forward, wavefield, preferred_element_type=jn...  24.3 us
    unnamed x12, local copies, waits for them, and re-layouts  18.3 us
    all_to_all x1, blocking collectives, per_device(): lax.all_to_all(bands, 'freq', split_axis=2, concat_axis=0, tiled=True)  9.97 us
    another operation x1, local copies, waits for them, and re-layouts, per_device(): jnp.stack([products[:, 0, 0] - products[:, 1, 1], products[:, 0, 1] + pro...  6.87 us
  transfers between devices with their start and end apart: 1, of which 0 were waited for; matrix products, arithmetic and copies ran while one was open for 18% of the time, Pallas kernels for 0%

commit v1 on v0

--- a/solution.py
+++ b/solution.py
@@ -3,10 +3,15 @@
 
 import jax
 import jax.numpy as jnp
+import numpy as np
 from jax import lax
+from jax.experimental import pallas as pl
+from jax.experimental.pallas import tpu as pltpu
 from jax.sharding import PartitionSpec as P
 
 RANK_MAX = 64
+MESH = pl.DeviceIdType.MESH
+LANES = 128
 
 
 def spectral_tables(freq_count, sample_count):
@@ -47,7 +52,7 @@
     return jnp.take(values, chosen, axis=1)
 
 
-def per_device(wavefield, u_factors, v_factors, tile_ranks, tile_offsets):
+def general_device(wavefield, u_factors, v_factors, tile_ranks, tile_offsets):
     rec_dev, src_dev, samples = wavefield.shape
     freq_dev = u_factors.shape[1]
     rows_dev = u_factors.shape[2]
@@ -112,6 +117,325 @@
     return series.astype(jnp.bfloat16).reshape(rows_dev * tile_size // freq_group, sources, samples)
 
 
+def host_tables(freq_count, sample_count):
+    freq_bins = np.arange(freq_count) + 1
+    phase = freq_bins[:, None] * np.arange(sample_count)[None, :] % sample_count
+    angles = phase * (2.0 * math.pi / sample_count)
+    stacked = np.stack([np.cos(angles), -np.sin(angles)], axis=1)
+    stacked = stacked.reshape(2 * freq_count, sample_count)
+    forward = (stacked / math.sqrt(sample_count)).astype(np.float32)
+    inverse = (stacked / math.sqrt(freq_count)).astype(np.float32)
+    return forward, inverse
+
+
+def band_kernel(
+    groups, chunks, tile, src_dev,
+    wave, table, u_ref, v_ref, starts, counts, out_ref,
+    wbuf, spec, send, xbuf, acc, bsend, brecv,
+    wsem, sa, ra, sx, rx, sp, rp, sq, rq, sb, rb,
+):
+    me = lax.axis_index("freq")
+    row = lax.axis_index("rows")
+    across = lax.rem(row + 2, 4)
+    partner = row + 1 - 2 * lax.rem(row, 2)
+    piece = send.shape[1] // groups
+    freq_dev = u_ref.shape[1]
+    slots = u_ref.shape[3]
+    chunk_rows = tile * src_dev
+
+    def load(c):
+        return pltpu.make_async_copy(
+            wave.at[pl.ds(c * chunk_rows, chunk_rows)], wbuf.at[c], wsem.at[c]
+        )
+
+    for c in range(chunks):
+        load(c).start()
+
+    barrier = pltpu.get_barrier_semaphore()
+
+    def greet(d, carry):
+        peer = lax.rem(me + d, groups)
+        pl.semaphore_signal(barrier, inc=1, device_id=(peer, row), device_id_type=MESH)
+        return carry
+
+    lax.fori_loop(1, groups, greet, 0)
+    pl.semaphore_signal(barrier, inc=1, device_id=(me, across), device_id_type=MESH)
+    pl.semaphore_signal(barrier, inc=1, device_id=(me, partner), device_id_type=MESH)
+    pl.semaphore_wait(barrier, groups + 1)
+
+    def exchange(c, peer, sender):
+        return pltpu.make_async_remote_copy(
+            src_ref=send.at[c, pl.ds(peer * piece, piece)],
+            dst_ref=xbuf.at[c, sender, row],
+            send_sem=sa.at[c, peer],
+            recv_sem=ra.at[c, sender],
+            device_id=(peer, row),
+            device_id_type=MESH,
+        )
+
+    def forward(c, g, block, target, s_sem, r_sem):
+        return pltpu.make_async_remote_copy(
+            src_ref=xbuf.at[c, g, block],
+            dst_ref=xbuf.at[c, g, block],
+            send_sem=s_sem.at[c, g],
+            recv_sem=r_sem.at[c, g],
+            device_id=(me, target),
+            device_id_type=MESH,
+        )
+
+    def to_across(c, g, block):
+        return forward(c, g, block, across, sx, rx)
+
+    def to_partner(c, g, block):
+        return forward(c, g, block, partner, sp, rp)
+
+    def to_partner_far(c, g, block):
+        return forward(c, g, block, partner, sq, rq)
+
+    acc[...] = jnp.zeros_like(acc)
+    lane_mod = lax.rem(lax.broadcasted_iota(jnp.int32, (tile, LANES), 1), src_dev)
+    sub = 512
+
+    def transform(c):
+        load(c).wait()
+
+        def block(b, carry):
+            rows = pl.ds(pl.multiple_of(b * sub, sub), sub)
+            values = lax.dot_general(
+                wbuf[c, rows, :], table[...], (((1,), (1,)), ((), ())),
+                preferred_element_type=jnp.float32,
+            )
+            for h in range(spec.shape[0]):
+                spec[h, rows, :] = values[:, h * LANES : (h + 1) * LANES]
+            return carry
+
+        lax.fori_loop(0, chunk_rows // sub, block, 0)
+        for h in range(spec.shape[0]):
+            cols = slice(h * LANES, (h + 1) * LANES)
+            picked = spec[h, pl.ds(0, tile, stride=src_dev), :]
+            for s in range(1, src_dev):
+                picked = jnp.where(
+                    lane_mod == s, spec[h, pl.ds(s, tile, stride=src_dev), :], picked
+                )
+            send[c, cols, :] = picked.T.astype(jnp.bfloat16)
+        own = pl.multiple_of(me * piece, piece)
+        xbuf[c, me, row] = send[c, pl.ds(own, piece), :]
+
+        def start(d, carry):
+            exchange(c, lax.rem(me + d, groups), me).start()
+            return carry
+
+        lax.fori_loop(1, groups, start, 0)
+        to_across(c, me, row).start()
+        to_partner(c, me, row).start()
+
+    def relay(c):
+        def step(d, carry):
+            g = lax.rem(me + groups - d, groups)
+            exchange(c, g, g).wait_recv()
+            to_across(c, g, row).start()
+            to_partner(c, g, row).start()
+            return carry
+
+        lax.fori_loop(1, groups, step, 0)
+
+    def relay_far(c):
+        def step(d, carry):
+            g = lax.rem(me + groups - d, groups)
+            to_across(c, g, across).wait_recv()
+            to_partner_far(c, g, across).start()
+            return carry
+
+        lax.fori_loop(0, groups, step, 0)
+
+    def project(c):
+        def arrive(d, carry):
+            g = lax.rem(me + groups - d, groups)
+            to_partner(c, g, partner).wait_recv()
+            to_partner_far(c, g, lax.rem(partner + 2, 4)).wait_recv()
+            return carry
+
+        lax.fori_loop(0, groups, arrive, 0)
+        slot = lax.broadcasted_iota(jnp.int32, (1, slots), 1)
+        half = 2 * src_dev
+        for k in range(freq_dev):
+            left = xbuf[c, :, :, k * half : (k + 1) * half, :].reshape(groups * 4 * half, tile)
+            for a in range(2):
+                products = lax.dot_general(
+                    left, v_ref[a, k], (((1,), (1,)), ((), ())),
+                    preferred_element_type=jnp.float32,
+                ).reshape(groups, 4 * half, slots)
+                total = acc[k, a]
+                for g in range(groups):
+                    first = starts[k, g * chunks + c]
+                    last = first + counts[k, g * chunks + c]
+                    inside = (slot >= first) & (slot < last)
+                    total = jnp.where(inside, products[g], total)
+                acc[k, a] = total
+
+    def step(c, carry):
+        pl.when(c < chunks)(lambda: transform(c))
+        pl.when((c >= 1) & (c < chunks + 1))(lambda: relay(c - 1))
+        pl.when((c >= 2) & (c < chunks + 2))(lambda: relay_far(c - 2))
+        pl.when(c >= 3)(lambda: project(c - 3))
+        return carry
+
+    lax.fori_loop(0, chunks + 3, step, 0)
+
+    rows_out = []
+    contract = (((1,), (1,)), ((), ()))
+    sources = 4 * src_dev
+    q_low = LANES // sources
+    q_high = tile // groups // q_low
+    for k in range(freq_dev):
+        first = acc[k, 0].reshape(4, 2, src_dev, slots)
+        second = acc[k, 1].reshape(4, 2, src_dev, slots)
+        real = (first[:, 0] - second[:, 1]).reshape(sources, slots)
+        imag = (first[:, 1] + second[:, 0]).reshape(sources, slots)
+        straight = jnp.concatenate([real, imag], axis=0).astype(jnp.bfloat16)
+        turned = jnp.concatenate([-imag, real], axis=0).astype(jnp.bfloat16)
+        band = lax.dot_general(u_ref[0, k], straight, contract, preferred_element_type=jnp.float32)
+        band = band + lax.dot_general(
+            u_ref[1, k], turned, contract, preferred_element_type=jnp.float32
+        )
+        split = band.reshape(groups, q_low, q_high, 2 * sources)
+        for part in range(2):
+            lanes = slice(part * sources, (part + 1) * sources)
+            rows_out.append(
+                jnp.concatenate([split[:, q, :, lanes] for q in range(q_low)], axis=-1)
+            )
+    bsend[...] = jnp.concatenate(rows_out, axis=1).astype(jnp.bfloat16)
+
+    def give_back(peer, sender):
+        return pltpu.make_async_remote_copy(
+            src_ref=bsend.at[peer],
+            dst_ref=brecv.at[sender],
+            send_sem=sb.at[peer],
+            recv_sem=rb.at[sender],
+            device_id=(peer, row),
+            device_id_type=MESH,
+        )
+
+    def start_back(d, carry):
+        give_back(lax.rem(me + d, groups), me).start()
+        return carry
+
+    lax.fori_loop(1, groups, start_back, 0)
+    brecv[me] = bsend[me]
+
+    def drain(c, carry):
+        def one(d, inner):
+            g = lax.rem(me + d, groups)
+            pl.when(d > 0)(lambda: exchange(c, g, me).wait_send())
+            to_across(c, g, row).wait_send()
+            to_partner(c, g, row).wait_send()
+            to_partner_far(c, g, across).wait_send()
+            return inner
+
+        return lax.fori_loop(0, groups, one, carry)
+
+    lax.fori_loop(0, chunks, drain, 0)
+
+    def finish(d, carry):
+        peer = lax.rem(me + d, groups)
+        give_back(peer, me).wait_send()
+        source = lax.rem(me + groups - d, groups)
+        give_back(source, source).wait_recv()
+        return carry
+
+    lax.fori_loop(1, groups, finish, 0)
+    out_ref[...] = brecv[...].reshape(out_ref.shape)
+
+
+def series_kernel(q_high, band_ref, table_ref, out_ref, wide):
+    step = pl.program_id(0)
+
+    @pl.when(step == 0)
+    def _():
+        wide[...] = band_ref[...].astype(jnp.float32)
+
+    left = wide[pl.ds(step, band_ref.shape[0] // q_high, stride=q_high), :]
+    series = jnp.dot(
+        left.T.astype(jnp.bfloat16), table_ref[...], preferred_element_type=jnp.float32
+    )
+    out_ref[...] = series.astype(jnp.bfloat16).reshape(out_ref.shape)
+
+
+def fast_device(wavefield, u_factors, v_factors, tile_ranks, tile_offsets):
+    rec_dev, src_dev, samples = wavefield.shape
+    freq_dev, tile, slots = u_factors.shape[1], u_factors.shape[3], u_factors.shape[4]
+    groups = lax.axis_size("freq")
+    chunks = rec_dev // tile
+    forward, inverse = host_tables(freq_dev * groups, samples)
+    table = jnp.asarray(np.repeat(forward, src_dev, axis=0)).astype(jnp.bfloat16)
+    inverse = jnp.asarray(inverse).astype(jnp.bfloat16)
+    columns = table.shape[0]
+    piece = columns // groups
+    sources = 4 * src_dev
+    q_dev = tile // groups
+    q_low = LANES // sources
+    q_high = q_dev // q_low
+    band_rows = 2 * freq_dev * q_high
+    vmem = pl.BlockSpec(memory_space=pltpu.VMEM)
+    smem = pl.BlockSpec(memory_space=pltpu.SMEM)
+    dma = pltpu.SemaphoreType.DMA
+    bands = pl.pallas_call(
+        functools.partial(band_kernel, groups, chunks, tile, src_dev),
+        out_shape=jax.ShapeDtypeStruct((groups * band_rows, LANES), jnp.bfloat16),
+        in_specs=[pl.BlockSpec(memory_space=pl.ANY), vmem, vmem, vmem, smem, smem],
+        out_specs=vmem,
+        scratch_shapes=[
+            pltpu.VMEM((chunks, tile * src_dev, samples), jnp.bfloat16),
+            pltpu.VMEM((columns // LANES, tile * src_dev, LANES), jnp.float32),
+            pltpu.VMEM((chunks, columns, tile), jnp.bfloat16),
+            pltpu.VMEM((chunks, groups, 4, piece, tile), jnp.bfloat16),
+            pltpu.VMEM((freq_dev, 2, 8 * src_dev, slots), jnp.float32),
+            pltpu.VMEM((groups, band_rows, LANES), jnp.bfloat16),
+            pltpu.VMEM((groups, band_rows, LANES), jnp.bfloat16),
+            dma((chunks,)),
+        ]
+        + [dma((chunks, groups)) for _ in range(8)]
+        + [dma((groups,)), dma((groups,))],
+        compiler_params=pltpu.CompilerParams(
+            collective_id=0, has_side_effects=True, vmem_limit_bytes=60 * 1024 * 1024
+        ),
+        name="bands",
+    )(
+        wavefield.reshape(rec_dev * src_dev, samples),
+        table,
+        u_factors[:, :, 0],
+        v_factors[:, :, 0],
+        tile_offsets[:, 0],
+        tile_ranks[:, 0],
+    )
+    series = pl.pallas_call(
+        functools.partial(series_kernel, q_high),
+        grid=(q_high,),
+        out_shape=jax.ShapeDtypeStruct((q_low, q_high, sources, samples), jnp.bfloat16),
+        in_specs=[
+            pl.BlockSpec(bands.shape, lambda q: (0, 0)),
+            pl.BlockSpec(inverse.shape, lambda q: (0, 0)),
+        ],
+        out_specs=pl.BlockSpec((q_low, 1, sources, samples), lambda q: (0, q, 0, 0)),
+        scratch_shapes=[pltpu.VMEM(bands.shape, jnp.float32)],
+        name="series",
+    )(bands, inverse)
+    return series.reshape(q_dev, sources, samples)
+
+
+def per_device(wavefield, u_factors, v_factors, tile_ranks, tile_offsets):
+    rec_dev, src_dev, samples = wavefield.shape
+    tile, slots = u_factors.shape[3], u_factors.shape[4]
+    groups = lax.axis_size("freq")
+    aligned = tile % LANES == 0 and rec_dev % tile == 0 and slots % LANES == 0
+    aligned = aligned and samples % LANES == 0
+    counts = u_factors.shape[1] == 2 and u_factors.shape[2] == 1 and src_dev == 8
+    counts = counts and lax.axis_size("rows") == 4 and groups > 1 and groups * 32 % LANES == 0
+    if aligned and counts and tile == groups * 32:
+        return fast_device(wavefield, u_factors, v_factors, tile_ranks, tile_offsets)
+    return general_device(wavefield, u_factors, v_factors, tile_ranks, tile_offsets)
+
+
 def solution(mesh):
     placed = (
         P("freq", "rows", None),

time: 296 us -> 48.4 us (0.16)
  local copies, waits for them, and re-layouts: 212 us -> 0 us
  Pallas kernels: 0 us -> 48.2 us
  blocking collectives: 34.9 us -> 0 us
  matrix products: 32.1 us -> 0 us
  between operations: 13.7 us -> 0.01 us
    reshape x2 -> x0, local copies, waits for them, and re-layouts: 79.3 us -> none  [the longest x1 74.5 us: per_device(): portion.reshape(blocks_in, freq_dev, 2, columns, tile_size, src_dev)]
    gather x5 -> x0, local copies, waits for them, and re-layouts: 57.9 us -> none  [the longest x3 51.3 us: tile_windows(): jnp.take(v_padded, slot_index, axis=1)]
    pallas_call x0 -> x2, Pallas kernels: none -> 48.2 us  [the longest x1 43.1 us: fast_device(): pl.pallas_call(functools.partial(band_kernel, groups, chunks, tile, src_d...]
    all_to_all x2 -> x0, blocking collectives: 34.9 us -> none  [the longest x1 24.9 us: per_device(): lax.all_to_all(spectrum, 'freq', split_axis=0, concat_axis=2, tiled=True)]
    dot_general x4 -> x0, matrix products: 32.1 us -> none  [the longest x1 24.3 us: per_device(): jnp.einsum('kct,rst->kcrs', forward, wavefield, preferred_element_type=jn...]
    transpose x2 -> x0, local copies, waits for them, and re-layouts: 31.3 us -> none  [the longest x1 30.3 us: per_device(): jnp.transpose(spectra, (1, 2, 3, 4, 0, 5))]
    unnamed x12 -> x0, local copies, waits for them, and re-layouts: 18.3 us -> none
    convert_element_type x2 -> x0, local copies, waits for them, and re-layouts: 8.58 us -> none  [the longest x1 4.52 us: per_device(): spectrum.astype(jnp.bfloat16).reshape(freqs, 2, rec_dev * src_dev)]
  transfers between devices with their start and end apart: 1 -> 0, of which waited for: 0 -> 0; matrix products, arithmetic and copies ran while one was open for 18% -> 0% of each run, Pallas kernels for 0% -> 0%
where the time goes in v1:
time: 48.4 us; the launch traced here: 48.2 us
  Pallas kernels  48.2 us (100%)
    pallas_call x1, Pallas kernels, fast_device(): pl.pallas_call(functools.partial(band_kernel, groups, chunks, tile, src_d...  43.1 us
    pallas_call x1, Pallas kernels, fast_device(): pl.pallas_call(functools.partial(series_kernel, q_high), grid=(q_high,),...  5.1 us

profile of v1, /device:TPU:0, one launch (start us, length us, event | category | flops | bytes accessed | tf_op | source)
XLA Modules:
  0.0 48.2 jit_solution(14537354269622048408)
XLA Ops:
  0.0 43.1 %bands.1.band_ref = bf16[256,128]{1,0:T(8,128)(2,1)} custom-call(bf16[10240,1024]{1,0:T(8,128)(2,1)} %bitcast.6, bf16[256,1024]{1,0:T(8,128)(2,1)} %constant.10.table, bf16[2,2,256,512]{3,2,1,0:T(8,128)(2,1)} %bitcast.7, bf16[2,2,512,256]{3,2,1,0:T(8,128)(2,1)} %bitcast.8, s32[2,40]{1,0:T(2,128)} %bitcast.9, s32[2,40]{1,0:T(2,128)} %bitcast.10), custom_call_target="tpu_custom_call" | custom-call | tf_op jit(solution)/shard_map/bands/pallas_call | solution.py:382
  43.1 5.1 %series.1 = bf16[4,8,32,1024]{3,2,1,0:T(8,128)(2,1)} custom-call(bf16[256,128]{1,0:T(8,128)(2,1)} %bands.1.band_ref, bf16[32,1024]{1,0:T(8,128)(2,1)} %constant.11.table_ref), custom_call_target="tpu_custom_call" | custom-call | tf_op jit(solution)/shard_map/series/pallas_call | solution.py:411

commit v2 on v1

--- a/solution.py
+++ b/solution.py
@@ -130,9 +130,9 @@
 
 def band_kernel(
     groups, chunks, tile, src_dev,
-    wave, table, u_ref, v_ref, starts, counts, out_ref,
-    wbuf, spec, send, xbuf, acc, bsend, brecv,
-    wsem, sa, ra, sx, rx, sp, rp, sq, rq, sb, rb,
+    wave, table, u_hbm, v_hbm, starts, counts, out_ref,
+    u_ref, v_ref, wbuf, spec, send, xbuf, acc, bsend, brecv,
+    usem, vsem, wsem, sa, ra, sx, rx, sp, rp, sq, rq, sb, rb,
 ):
     me = lax.axis_index("freq")
     row = lax.axis_index("rows")
@@ -150,6 +150,10 @@
 
     for c in range(chunks):
         load(c).start()
+    load_v = pltpu.make_async_copy(v_hbm, v_ref, vsem)
+    load_u = pltpu.make_async_copy(u_hbm, u_ref, usem)
+    load_v.start()
+    load_u.start()
 
     barrier = pltpu.get_barrier_semaphore()
 
@@ -194,7 +198,7 @@
 
     acc[...] = jnp.zeros_like(acc)
     lane_mod = lax.rem(lax.broadcasted_iota(jnp.int32, (tile, LANES), 1), src_dev)
-    sub = 512
+    sub = 2048
 
     def transform(c):
         load(c).wait()
@@ -202,7 +206,7 @@
         def block(b, carry):
             rows = pl.ds(pl.multiple_of(b * sub, sub), sub)
             values = lax.dot_general(
-                wbuf[c, rows, :], table[...], (((1,), (1,)), ((), ())),
+                wbuf[c, rows, :], table[...], (((1,), (0,)), ((), ())),
                 preferred_element_type=jnp.float32,
             )
             for h in range(spec.shape[0]):
@@ -275,13 +279,15 @@
 
     def step(c, carry):
         pl.when(c < chunks)(lambda: transform(c))
-        pl.when((c >= 1) & (c < chunks + 1))(lambda: relay(c - 1))
-        pl.when((c >= 2) & (c < chunks + 2))(lambda: relay_far(c - 2))
-        pl.when(c >= 3)(lambda: project(c - 3))
+        pl.when((c >= 2) & (c < chunks + 2))(lambda: relay(c - 2))
+        pl.when((c >= 3) & (c < chunks + 3))(lambda: relay_far(c - 3))
+        pl.when(c == 4)(load_v.wait)
+        pl.when(c >= 4)(lambda: project(c - 4))
         return carry
 
-    lax.fori_loop(0, chunks + 3, step, 0)
-
+    lax.fori_loop(0, chunks + 4, step, 0)
+
+    load_u.wait()
     rows_out = []
     contract = (((1,), (1,)), ((), ()))
     sources = 4 * src_dev
@@ -354,11 +360,14 @@
     def _():
         wide[...] = band_ref[...].astype(jnp.float32)
 
-    left = wide[pl.ds(step, band_ref.shape[0] // q_high, stride=q_high), :]
-    series = jnp.dot(
-        left.T.astype(jnp.bfloat16), table_ref[...], preferred_element_type=jnp.float32
-    )
-    out_ref[...] = series.astype(jnp.bfloat16).reshape(out_ref.shape)
+    q_low, q_step, sources, samples = out_ref.shape
+    for q in range(q_step):
+        rows = pl.ds(step * q_step + q, band_ref.shape[0] // q_high, stride=q_high)
+        series = jnp.dot(
+            wide[rows, :].T.astype(jnp.bfloat16), table_ref[...],
+            preferred_element_type=jnp.float32,
+        )
+        out_ref[:, q] = series.astype(jnp.bfloat16).reshape(q_low, sources, samples)
 
 
 def fast_device(wavefield, u_factors, v_factors, tile_ranks, tile_offsets):
@@ -367,24 +376,28 @@
     groups = lax.axis_size("freq")
     chunks = rec_dev // tile
     forward, inverse = host_tables(freq_dev * groups, samples)
-    table = jnp.asarray(np.repeat(forward, src_dev, axis=0)).astype(jnp.bfloat16)
+    table = jnp.asarray(np.repeat(forward.T, src_dev, axis=1)).astype(jnp.bfloat16)
     inverse = jnp.asarray(inverse).astype(jnp.bfloat16)
-    columns = table.shape[0]
+    columns = table.shape[1]
     piece = columns // groups
     sources = 4 * src_dev
     q_dev = tile // groups
     q_low = LANES // sources
     q_high = q_dev // q_low
+    q_step = q_high // math.gcd(q_high, 2)
     band_rows = 2 * freq_dev * q_high
     vmem = pl.BlockSpec(memory_space=pltpu.VMEM)
+    hbm = pl.BlockSpec(memory_space=pl.ANY)
     smem = pl.BlockSpec(memory_space=pltpu.SMEM)
     dma = pltpu.SemaphoreType.DMA
     bands = pl.pallas_call(
         functools.partial(band_kernel, groups, chunks, tile, src_dev),
         out_shape=jax.ShapeDtypeStruct((groups * band_rows, LANES), jnp.bfloat16),
-        in_specs=[pl.BlockSpec(memory_space=pl.ANY), vmem, vmem, vmem, smem, smem],
+        in_specs=[hbm, vmem, hbm, hbm, smem, smem],
         out_specs=vmem,
         scratch_shapes=[
+            pltpu.VMEM((2, freq_dev, tile, slots), jnp.bfloat16),
+            pltpu.VMEM((2, freq_dev, slots, tile), jnp.bfloat16),
             pltpu.VMEM((chunks, tile * src_dev, samples), jnp.bfloat16),
             pltpu.VMEM((columns // LANES, tile * src_dev, LANES), jnp.float32),
             pltpu.VMEM((chunks, columns, tile), jnp.bfloat16),
@@ -392,6 +405,8 @@
             pltpu.VMEM((freq_dev, 2, 8 * src_dev, slots), jnp.float32),
             pltpu.VMEM((groups, band_rows, LANES), jnp.bfloat16),
             pltpu.VMEM((groups, band_rows, LANES), jnp.bfloat16),
+            dma,
+            dma,
             dma((chunks,)),
         ]
         + [dma((chunks, groups)) for _ in range(8)]
@@ -410,13 +425,13 @@
     )
     series = pl.pallas_call(
         functools.partial(series_kernel, q_high),
-        grid=(q_high,),
+        grid=(q_high // q_step,),
         out_shape=jax.ShapeDtypeStruct((q_low, q_high, sources, samples), jnp.bfloat16),
         in_specs=[
             pl.BlockSpec(bands.shape, lambda q: (0, 0)),
             pl.BlockSpec(inverse.shape, lambda q: (0, 0)),
         ],
-        out_specs=pl.BlockSpec((q_low, 1, sources, samples), lambda q: (0, q, 0, 0)),
+        out_specs=pl.BlockSpec((q_low, q_step, sources, samples), lambda q: (0, q, 0, 0)),
         scratch_shapes=[pltpu.VMEM(bands.shape, jnp.float32)],
         name="series",
     )(bands, inverse)

time: 48.4 us -> 43.3 us (0.89)
  Pallas kernels: 48.2 us -> 43.1 us
    pallas_call x1, Pallas kernels: 43.1 us -> 40.3 us  [fast_device(): pl.pallas_call(functools.partial(band_kernel, groups, chunks, tile, src_d...]
    pallas_call x1, Pallas kernels: 5.1 us -> 2.86 us  [fast_device(): pl.pallas_call(functools.partial(series_kernel, q_high), grid=(q_high //...]
where the time goes in v2:
time: 43.3 us; the launch traced here: 43.1 us
  Pallas kernels  43.1 us (100%)
    pallas_call x1, Pallas kernels, fast_device(): pl.pallas_call(functools.partial(band_kernel, groups, chunks, tile, src_d...  40.3 us
    pallas_call x1, Pallas kernels, fast_device(): pl.pallas_call(functools.partial(series_kernel, q_high), grid=(q_high //...  2.86 us

profile of v2, /device:TPU:0, one launch (start us, length us, event | category | flops | bytes accessed | tf_op | source)
XLA Modules:
  0.0 43.1 jit_solution(5796317490827979005)
XLA Ops:
  0.0 40.3 %bands.1.band_ref = bf16[256,128]{1,0:T(8,128)(2,1)} custom-call(bf16[10240,1024]{1,0:T(8,128)(2,1)} %bitcast.6, bf16[1024,256]{1,0:T(8,128)(2,1)} %constant.10.table, bf16[2,2,256,512]{3,2,1,0:T(8,128)(2,1)} %bitcast.7, bf16[2,2,512,256]{3,2,1,0:T(8,128)(2,1)} %bitcast.8, s32[2,40]{1,0:T(2,128)} %bitcast.9, s32[2,40]{1,0:T(2,128)} %bitcast.10), custom_call_target="tpu_custom_call" | custom-call | tf_op jit(solution)/shard_map/bands/pallas_call | solution.py:393
  40.3 2.9 %series.1 = bf16[4,8,32,1024]{3,2,1,0:T(8,128)(2,1)} custom-call(bf16[256,128]{1,0:T(8,128)(2,1)} %bands.1.band_ref, bf16[32,1024]{1,0:T(8,128)(2,1)} %constant.11.table_ref), custom_call_target="tpu_custom_call" | custom-call | tf_op jit(solution)/shard_map/series/pallas_call | solution.py:426
